TPU v7x, 1024 devices: a whole 8x8x8 slice. The times are simulated.
1024 devices in a mesh: ctx: 64 (over y, x), tp: 8 (over z), grp: 2 (over core).
Axes of the slice: x: 8, y: 8, z: 8, core: 2. Of those that a mesh axis runs over, the one named last changes fastest.
Arguments:
- patches: bfloat16 [8192, 5120], P('ctx'), may hold values from -6 to 6
- route_count: int32 [64, 64], replicated, may hold values from 0 to 2, as said below
- text_states: bfloat16 [8192, 4096], P('ctx', ('tp', 'grp')), may hold values from -6 to 6
- segment_ids: int32 [8192], replicated, may hold values from 0 to 3, never falling along the last dimension, each value on 1 to 4096 neighbouring positions
- vision_gain: float32 [1280], replicated, may hold values from 0.1 to 1.9
- merge_up: bfloat16 [5120, 2560], P(None, ('tp', 'grp')), may hold values from -0.078125 to 0.078125
- merge_down: bfloat16 [2560, 4096], P(('tp', 'grp')), may hold values from -0.125 to 0.125
- norm_gain: float32 [4096], replicated, may hold values from 0.1 to 1.9
- query_weight: bfloat16 [4096, 4096], P(None, ('tp', 'grp')), may hold values from -0.62928387 to 0.62928387
- kv_weight: bfloat16 [4096, 2048], P(None, 'tp'), may hold values from -0.4578688 to 0.4578688
Outputs:
- attended: bfloat16 [8192, 4096], P('ctx', ('tp', 'grp'))
Inputs may be any that keep to these rules, and one draw needn't show every extreme that they name: route_count[c, d] counts the live rows among the 2 rows that source c holds for owner d; at least one owner gets 2 live rows from every source. `segment_ids`: never falling along the packed batch; a segment has at most 4096 positions.
All inputs are finite; a program needn't handle non-finite values.
Results may differ from a plain program's by a relative error of at most 0.04.
Values may be sent and summed in bfloat16 or wider, within the bound.
No kernel may reach another device: no remote copies, remote signals or barrier semaphores. Data moves between devices by JAX's collectives and lax.ppermute only.
A program may use at most 64 MiB of HBM per device.

v0:
```python
import jax
import jax.numpy as jnp
from jax import lax
from jax.sharding import Mesh
from jax.sharding import PartitionSpec as P

HD = 128
CTX = ("ctx_0", "ctx_1")


EPSILON = 1e-06
NEGATIVE = -1e30


def in_blocks(shard, dim, length):
    lengths = shard.shape
    parts = shard.reshape(*lengths[:dim], length, lengths[dim] // length, *lengths[dim + 1 :])
    return jnp.moveaxis(parts, dim, 0)


def sum_at_owner(shard, axis, dim):
    parts = in_blocks(shard, dim, lax.axis_size(axis))
    arrived = lax.all_to_all(parts, axis, split_axis=0, concat_axis=0, tiled=True)
    return arrived.sum(axis=0)


def from_everyone(shard, axis):
    length = lax.axis_size(axis)
    return lax.all_to_all(
        jnp.broadcast_to(shard[None], (length, *shard.shape)), axis, 0, 0, tiled=True
    )


def in_order(parts, dim):
    lengths = list(parts.shape[1:])
    lengths[dim] *= parts.shape[0]
    return jnp.moveaxis(parts, 0, dim).reshape(lengths)


def collect(shard, axis, dim):
    parts = from_everyone(shard, axis)
    return in_order(parts, dim)


def gather_in_order(shard, axes, turns):
    parts = shard[None]
    for k in turns:
        parts = lax.all_gather(parts, axes[k], axis=0, tiled=True)
    block = [lax.axis_size(axes[k]) for k in reversed(turns)]
    parts = parts.reshape(*block, *shard.shape)
    turned = sorted(range(len(turns)), key=lambda place: turns[len(turns) - 1 - place])
    return parts.transpose(*turned, *range(len(turns), parts.ndim)).reshape(-1, *shard.shape)


def gather_axes(shard, axes, turns, dim):
    return in_order(gather_in_order(shard, axes, turns), dim)


def rms_scale(values, gain):
    mean_square = jnp.mean(values * values, axis=-1, keepdims=True)
    return values * lax.rsqrt(mean_square + EPSILON) * gain


def attend(
    running,
    queries4,
    shard_piece,
    key_pos,
    query_pos,
    query_seg,
    segment_ids,
    visual_count,
    tokens_dev,
):
    weighted, running_max, denominator = running
    piece_rows = shard_piece.shape[0]
    kv_heads = queries4.shape[1]
    kv_split = shard_piece.reshape(piece_rows, kv_heads, 2, HD)
    key_block = kv_split[:, :, 0]
    value_block = kv_split[:, :, 1]
    key_owner = key_pos // tokens_dev
    owner_match = key_owner[:, None] == jnp.arange(visual_count.shape[0], dtype=jnp.int32)[None, :]
    visual_limit = jnp.sum(jnp.where(owner_match, visual_count[None, :], 0), axis=1)
    key_visual = key_pos % tokens_dev < visual_limit
    key_seg = segment_ids[key_pos]
    allowed = (query_seg[:, None] == key_seg[None, :]) & (
        key_visual[None, :] | (key_pos[None, :] <= query_pos[:, None])
    )
    scores = jnp.where(
        allowed,
        jnp.einsum("qkgd,rkd->kgqr", queries4, key_block, preferred_element_type=jnp.float32)
        * HD ** (-0.5),
        NEGATIVE,
    )
    new_max = jnp.maximum(running_max, jnp.max(scores, axis=-1))
    weights = jnp.exp(jnp.where(allowed, scores - new_max[..., None], NEGATIVE))
    denominator = jnp.sum(weights, axis=-1)
    weighted = jnp.einsum(
        "kgqr,rkd->kgqd",
        weights.astype(jnp.bfloat16),
        value_block,
        preferred_element_type=jnp.float32,
    )
    return (weighted, new_max, denominator)


def start_state(kv_heads, per_head, tokens_dev):
    return (
        jnp.zeros((kv_heads, per_head, tokens_dev, HD), jnp.float32),
        jnp.full((kv_heads, per_head, tokens_dev), NEGATIVE, jnp.float32),
        jnp.zeros((kv_heads, per_head, tokens_dev), jnp.float32),
    )


def shards(
    patches,
    route_count,
    text_states,
    segment_ids,
    vision_gain,
    merge_up,
    merge_down,
    norm_gain,
    query_weight,
    kv_weight,
):
    ctx_size = lax.axis_size(CTX)
    owner_index = lax.axis_index(CTX)
    row_count = patches.shape[0]
    bucket_rows = row_count // ctx_size
    tokens_dev = text_states.shape[0]
    grouped = patches.astype(jnp.float32).reshape(row_count, 4, -1)
    patch_normed = rms_scale(grouped, vision_gain).reshape(row_count, -1).astype(jnp.bfloat16)
    hidden = jax.nn.gelu(
        jnp.dot(patch_normed, merge_up, preferred_element_type=jnp.float32), approximate=False
    ).astype(jnp.bfloat16)
    partial_value = jnp.dot(hidden, merge_down, preferred_element_type=jnp.float32)
    column = lax.dynamic_slice_in_dim(route_count, owner_index, 1, 1)[:, 0]
    count_ends = jnp.cumsum(column)
    count_starts = count_ends - column
    slot_ids = jnp.arange(tokens_dev, dtype=jnp.int32)
    source = jnp.sum((count_ends[None, :] <= slot_ids[:, None]).astype(jnp.int32), axis=1)
    source = jnp.minimum(source, ctx_size - 1)
    source_match = source[:, None] == jnp.arange(ctx_size, dtype=jnp.int32)[None, :]
    first_slot = jnp.sum(jnp.where(source_match, count_starts[None, :], 0), axis=1)
    visual = slot_ids < count_ends[ctx_size - 1]
    pick_rows = jnp.where(visual, source * bucket_rows + slot_ids - first_slot, 0)
    merged_part = sum_at_owner(partial_value, ("tp", "grp"), 1).astype(jnp.bfloat16)
    arrived = lax.all_to_all(
        merged_part.reshape(ctx_size, bucket_rows, -1), CTX, split_axis=0, concat_axis=0, tiled=True
    )
    arrived = arrived.reshape(row_count, -1)
    placed = jnp.where(visual[:, None], arrived[pick_rows], text_states)
    packed = collect(placed, ("tp", "grp"), 1)
    normal = rms_scale(packed.astype(jnp.float32), norm_gain).astype(jnp.bfloat16)
    queries = jnp.dot(normal, query_weight, preferred_element_type=jnp.float32).astype(jnp.bfloat16)
    kv_pairs = jnp.dot(normal, kv_weight, preferred_element_type=jnp.float32).astype(jnp.bfloat16)
    heads_dev = queries.shape[1] // HD
    query_pos = owner_index * tokens_dev + slot_ids
    query_seg = segment_ids[query_pos]
    visual_count = jnp.sum(route_count, axis=0)
    queries4 = queries.reshape(tokens_dev, 1, heads_dev, HD)
    shard_piece = gather_axes(kv_pairs, CTX, (0, 1), 0)
    key_pos = jnp.arange(shard_piece.shape[0], dtype=jnp.int32)
    weighted, running_max, denominator = attend(
        start_state(1, heads_dev, tokens_dev),
        queries4,
        shard_piece,
        key_pos,
        query_pos,
        query_seg,
        segment_ids,
        visual_count,
        tokens_dev,
    )
    result = (weighted / denominator[..., None]).reshape(heads_dev, tokens_dev, HD)
    return result.transpose(1, 0, 2).reshape(tokens_dev, -1).astype(jnp.bfloat16)


def solution(mesh):
    finer = Mesh(
        mesh.devices.reshape(8, 8, mesh.shape["tp"], mesh.shape["grp"]),
        ("ctx_0", "ctx_1", "tp", "grp"),
    )
    return jax.shard_map(
        shards,
        mesh=finer,
        in_specs=(
            P(CTX, None),
            P(),
            P(CTX, ("tp", "grp")),
            P(),
            P(),
            P(None, ("tp", "grp")),
            P(("tp", "grp"), None),
            P(),
            P(None, ("tp", "grp")),
            P(None, "tp"),
        ),
        out_specs=P(CTX, ("tp", "grp")),
        check_vma=False,
    )
```

profile of v0, /device:TPU:1, one launch (start us, length us, event | category | flops | bytes accessed | tf_op | source)
XLA Modules:
  0.0 264.0 jit_solution(5487455328636447750)
XLA Ops:
  6.5 0.8 mul.107
  7.4 3.1 %convert_multiply_fusion.1 = f32[128,5120]{1,0:T(8,128)} fusion(bf16[128,5120]{1,0:T(8,128)(2,1)} %param.10), kind=kLoop, calls=%fused_computation.18 | loop fusion | flops 1310720 | bytes 3932160 | tf_op jit(solution)/shard_map/mul | solution.py:60
  10.5 4.0 %mul.103 = f32[128,4,1280]{2,1,0:T(4,128)} reshape(f32[128,5120]{1,0:T(8,128)} %convert_multiply_fusion.1) | data formatting | bytes 5242880 | tf_op jit(solution)/shard_map/mul | solution.py:60
  14.5 2.2 reduce_sum.76
  17.1 2.0 copy.61
  19.0 5.6 %fusion.42 = f32[128,4096]{1,0:T(8,128)} fusion(bf16[160,4096]{1,0:T(8,128)(2,1)} %param.16, bf16[5120,160]{0,1:T(8,128)(2,1)} %param.15, f32[128,5120]{1,0:T(8,128)} %bitcast.98, bf16[128,5120]{1,0:T(8,128)(2,1)S(1)} %copy-done.2, f32[5120]{0:T(1024)S(1)} %mul.108), kind=kOutput, calls=%fused_computation.57 | convolution fusion | flops 381440000 | bytes 8998912 | tf_op jit(solution)/shard_map/dot_general | solution.py:137
  24.7 3.2 %copy.70 = f32[16,16,8,256]{3,2,0,1:T(8,128)} copy(f32[16,16,8,256]{3,2,1,0:T(8,128)} %bitcast.100) | data formatting | bytes 4194304 | tf_op jit(solution)/shard_map/reshape | solution.py:17
  27.8 18.4 %all-to-all-start = ((f32[16,128,256]{2,1,0:T(8,128)}), f32[16,128,256]{2,1,0:T(8,128)}, u32[]{:S(2)}, u32[]{:S(2)}) async-start(f32[16,128,256]{2,1,0:T(8,128)} %bitcast.99), calls=%async_computation | async-start | bytes 4194304 | tf_op jit(solution)/shard_map/all_to_all | solution.py:23
  46.6 0.5 slice.19
  47.4 0.6 fusion.83
  48.0 47.4 %all-to-all-done = f32[16,128,256]{2,1,0:T(8,128)} async-done(((f32[16,128,256]{2,1,0:T(8,128)}), f32[16,128,256]{2,1,0:T(8,128)}, u32[]{:S(2)}, u32[]{:S(2)}) %all-to-all-start) | async-done | bytes 2097184 | tf_op jit(solution)/shard_map/all_to_all | solution.py:23
  95.5 1.7 reduce_sum.77
  97.2 0.7 convert_element_type.54
  97.9 13.1 %all-to-all-start.1 = ((bf16[64,2,256]{2,1,0:T(2,128)(2,1)}), bf16[64,2,256]{2,1,0:T(2,128)(2,1)S(1)}, u32[]{:S(2)}, u32[]{:S(2)}) async-start(bf16[64,2,256]{2,1,0:T(2,128)(2,1)} %convert_element_type.54), calls=%async_computation.1 | async-start | bytes 131072 | tf_op jit(solution)/shard_map/all_to_all | solution.py:149
  111.0 0.6 iota_compare_fusion.4
  111.6 10.4 %all-to-all-done.1 = bf16[64,2,256]{2,1,0:T(2,128)(2,1)S(1)} async-done(((bf16[64,2,256]{2,1,0:T(2,128)(2,1)}), bf16[64,2,256]{2,1,0:T(2,128)(2,1)S(1)}, u32[]{:S(2)}, u32[]{:S(2)}) %all-to-all-start.1) | async-done | bytes 65568 | tf_op jit(solution)/shard_map/all_to_all | solution.py:149
  122.0 0.8 gather_fusion.2
  123.3 34.5 %all_to_all.15 = bf16[16,128,256]{1,2,0:T(8,128)(2,1)S(1)} all-to-all(bf16[16,128,256]{1,2,0:T(8,128)(2,1)S(1)} %broadcast_in_dim.56), channel_id=1, replica_groups=mesh['ctx_0'=8,'ctx_1'=8,'tp'=8,'grp'=2] {'tp','grp'}, dimensions={0} | all-to-all | bytes 2097152 | tf_op jit(solution)/shard_map/all_to_all | solution.py:29
  157.8 0.6 multiply_reduce_fusion
  158.4 0.7 fusion.15
  159.1 0.6 convolution_convert_fusion.1
  159.7 21.6 %all-gather = bf16[1024,256]{1,0:T(8,128)(2,1)} all-gather(bf16[128,256]{1,0:T(8,128)(2,1)S(1)} %convolution_convert_fusion.1), channel_id=2, replica_groups=mesh['ctx_0'=8,'ctx_1'=8,'tp'=8,'grp'=2] {'ctx_0'}, dimensions={0}, use_global_device_ids=true | all-gather | bytes 589824 | tf_op jit(solution)/shard_map/all_gather | solution.py:48
  181.4 1.1 gather_fusion
  182.6 45.5 %gather_fusion.1 = s32[8192]{0:T(1024)S(1)} fusion(s32[8192]{0:T(1024)S(1)} %copy-done.1, s32[8192]{0:T(1024)S(1)} %iota_clamp_fusion), kind=kCustom, calls=%fused_computation.1 | custom fusion | bytes 98304 | tf_op jit(solution)/shard_map/gather | solution.py:85
  228.6 4.3 %fusion.10 = pred[128,8192]{0,1:T(8,128)(4,1)} fusion(s32[128]{0:T(128)S(1)} %iota_add_fusion, s32[128]{0:T(128)S(1)} %gather_fusion, s32[8192]{0:T(1024)S(1)} %gather_fusion.1, pred[8192]{0:T(1024)(128)(4,1)S(1)} %fusion.76), kind=kLoop, calls=%fused_computation.15 | loop fusion | flops 4194304 | bytes 1090560 | tf_op jit(solution)/shard_map/and | solution.py:86
  232.9 2.2 fusion.22
  235.1 6.6 %copy.52 = bf16[8,8,128,256]{2,1,0,3:T(8,128)(2,1)} copy(bf16[8,8,128,256]{3,2,0,1:T(8,128)(2,1)} %bitcast.101) | data formatting | bytes 8388608 | tf_op jit(solution)/shard_map/transpose | solution.py:52
  241.7 7.4 %reshape_reshape_reshape.3 = bf16[8192,1,2,128]{0,3,2,1:T(8,128)(2,1)} reshape(bf16[8,8,128,256]{2,1,0,3:T(8,128)(2,1)} %copy.52) | data formatting | bytes 8388608 | tf_op jit(solution)/shard_map/reshape;reshape;reshape | solution.py:78
  249.1 3.4 %fusion.116 = (f32[2,128]{1,0:T(2,128)S(1)}, f32[1,2,128,8192]{2,3,1,0:T(8,128)S(1)}) fusion(bf16[16,2,8,128]{3,2,1,0:T(8,128)(2,1)S(1)} %fusion.22, bf16[8192,1,2,128]{0,3,2,1:T(8,128)(2,1)} %reshape_reshape_reshape.3, pred[128,8192]{0,1:T(8,128)(4,1)S(1)} %copy-done.3), kind=kOutput, calls=%fused_computation.155 | convolution fusion | flops 543162112 | bytes 11600896 | tf_op jit(solution)/shard_map/qkgd,rkd->kgqr/dot_general | solution.py:91
  252.5 1.7 fusion.2
  254.7 1.8 fusion.26
  256.5 0.7 copy.56
  (44 shorter events, 2.5 us)
Async XLA Ops:
  6.5 152.6 %copy-start = (bf16[4096,256]{1,0:T(8,128)(2,1)S(1)}, bf16[4096,256]{1,0:T(8,128)(2,1)}, u32[]{:S(2)}) copy-start(bf16[4096,256]{1,0:T(8,128)(2,1)} %param.19) | copy-start | bytes 6291460
  17.1 2.0 copy-start.2
  27.8 18.4 %copy-start.5 = (s32[64,64]{1,0:T(8,128)S(1)}, s32[64,64]{1,0:T(8,128)}, u32[]{:S(2)}) copy-start(s32[64,64]{1,0:T(8,128)} %param.11) | copy-start | bytes 49156
  27.8 67.6 %all-to-all-start = ((f32[16,128,256]{2,1,0:T(8,128)}), f32[16,128,256]{2,1,0:T(8,128)}, u32[]{:S(2)}, u32[]{:S(2)}) async-start(f32[16,128,256]{2,1,0:T(8,128)} %bitcast.99), calls=%async_computation | async-start | bytes 4194304 | tf_op jit(solution)/shard_map/all_to_all | solution.py:23
  46.3 76.6 %copy-start.6 = (bf16[128,256]{1,0:T(8,128)(2,1)S(1)}, bf16[128,256]{1,0:T(8,128)(2,1)}, u32[]{:S(2)}) copy-start(bf16[128,256]{1,0:T(8,128)(2,1)} %param.12) | copy-start | bytes 196612
  97.9 24.1 %all-to-all-start.1 = ((bf16[64,2,256]{2,1,0:T(2,128)(2,1)}), bf16[64,2,256]{2,1,0:T(2,128)(2,1)S(1)}, u32[]{:S(2)}, u32[]{:S(2)}) async-start(bf16[64,2,256]{2,1,0:T(2,128)(2,1)} %convert_element_type.54), calls=%async_computation.1 | async-start | bytes 131072 | tf_op jit(solution)/shard_map/all_to_all | solution.py:149
  110.9 124.2 %all-gather.3.cloned.1.call-start = ((), (), s32[]{:S(2)}) async-start(), calls=%async_computation.3 | async-start | bytes 4718592 | tf_op jit(solution)/shard_map/all_gather | solution.py:48
  123.1 35.3 %copy-start.7 = (f32[4096]{0:T(1024)S(1)}, f32[4096]{0:T(1024)}, u32[]{:S(2)}) copy-start(f32[4096]{0:T(1024)} %param.17) | copy-start | bytes 49156
  159.1 22.3 %copy-start.1 = (s32[8192]{0:T(1024)S(1)}, s32[8192]{0:T(1024)}, u32[]{:S(2)}) copy-start(s32[8192]{0:T(1024)} %param.13) | copy-start | bytes 98308
  241.7 7.4 %copy-start.3 = (pred[128,8192]{0,1:T(8,128)(4,1)S(1)}, pred[128,8192]{0,1:T(8,128)(4,1)}, u32[]{:S(2)}) copy-start(pred[128,8192]{0,1:T(8,128)(4,1)} %fusion.10) | copy-start | bytes 3145732
  252.5 2.2 copy-start.4
Sparse Core Ops, SparseCore 0:
  181.5 53.0 all-gather.2
where the time goes:
time: 268 us; the launch traced here: 264 us
  local copies, waits for them, and re-layouts  74.8 us (28%)
  waiting for transfers between devices  57.9 us (22%)
  blocking collectives  56.1 us (21%)
  starting transfers between devices  31.5 us (12%)
  other arithmetic  16.5 us (6%)
  between operations  13.7 us (5%)
  matrix products  13.5 us (5%)
    all_to_all x1, waiting for transfers between devices, sum_at_owner(): lax.all_to_all(parts, axis, split_axis=0, concat_axis=0, tiled=True)  47.4 us
    gather x1, local copies, waits for them, and re-layouts, attend(): key_seg = segment_ids[key_pos]  45.5 us
    all_to_all x1, blocking collectives, from_everyone(): lax.all_to_all(jnp.broadcast_to(shard[None], (length, *shard.shape)), axi...  34.5 us
    all_gather x1, blocking collectives, gather_in_order(): parts = lax.all_gather(parts, axes[k], axis=0, tiled=True)  21.6 us
    all_to_all x1, starting transfers between devices, sum_at_owner(): lax.all_to_all(parts, axis, split_axis=0, concat_axis=0, tiled=True)  18.4 us
    all_to_all x1, starting transfers between devices, shards(): lax.all_to_all(merged_part.reshape(ctx_size, bucket_rows, -1), CTX, split...  13.1 us
    all_to_all x1, waiting for transfers between devices, shards(): lax.all_to_all(merged_part.reshape(ctx_size, bucket_rows, -1), CTX, split...  10.4 us
    another operation x1, local copies, waits for them, and re-layouts, attend(): kv_split = shard_piece.reshape(piece_rows, kv_heads, 2, HD)  7.4 us
  transfers between devices with their start and end apart: 3, of which 2 were waited for; matrix products, arithmetic and copies ran while one was open for 21% of the time, Pallas kernels for 0%

commit v1 on v0

v1 whole, which is shorter than its diff:
```python
import functools

import jax
import jax.numpy as jnp
from jax import lax
from jax.experimental import pallas as pl
from jax.experimental.pallas import tpu as pltpu
from jax.sharding import Mesh
from jax.sharding import PartitionSpec as P

HD = 128
EPSILON = 1e-06
NEGATIVE = -1e30
LOG2E = 1.4426950408889634
F32 = jnp.float32
BF16 = jnp.bfloat16
VMEM = pl.BlockSpec(memory_space=pltpu.VMEM)
SMEM = pl.BlockSpec(memory_space=pltpu.SMEM)


def params(*semantics):
    return pltpu.CompilerParams(
        dimension_semantics=semantics or None, vmem_limit_bytes=40 << 20
    )


def exchange(parts, axis, dim=0):
    return lax.all_to_all(parts, axis, split_axis=dim, concat_axis=dim, tiled=True)


def up_kernel(x_ref, gain_ref, w_ref, out_ref, acc_ref):
    step = pl.program_id(0)
    x = x_ref[...].astype(F32)
    scale = lax.rsqrt(jnp.mean(x * x, axis=-1, keepdims=True) + EPSILON)
    normed = (x * scale * gain_ref[...]).astype(BF16)
    product = jnp.dot(normed, w_ref[...], preferred_element_type=F32)

    @pl.when(step == 0)
    def _():
        acc_ref[...] = product

    @pl.when(step > 0)
    def _():
        acc_ref[...] += product

    @pl.when(step == pl.num_programs(0) - 1)
    def _():
        total = acc_ref[...]
        out_ref[...] = (0.5 * total * (1.0 + lax.erf(total * 0.5**0.5))).astype(BF16)


def merge_up_rows(patches, vision_gain, merge_up):
    rows, width = patches.shape
    vis = vision_gain.shape[0]
    units = merge_up.shape[1]
    return pl.pallas_call(
        up_kernel,
        grid=(width // vis,),
        in_specs=[
            pl.BlockSpec((rows, vis), lambda k: (0, k)),
            pl.BlockSpec((1, vis), lambda k: (0, 0)),
            pl.BlockSpec((vis, units), lambda k: (k, 0)),
        ],
        out_specs=pl.BlockSpec((rows, units), lambda k: (0, 0)),
        out_shape=jax.ShapeDtypeStruct((rows, units), BF16),
        scratch_shapes=[pltpu.VMEM((rows, units), F32)],
        compiler_params=params("arbitrary"),
        name="merge_up",
    )(patches, vision_gain.reshape(1, vis), merge_up)


def owner_column(owner, route):
    lanes = lax.broadcasted_iota(jnp.int32, route.shape, 1)
    return jnp.sum(jnp.where(lanes == owner, route, 0), axis=1, keepdims=True)


def down_kernel(owner_ref, route_ref, arrived_ref, w_ref, out_ref, pick_ref):
    step = pl.program_id(0)

    @pl.when(step == 0)
    def _():
        rows = arrived_ref.shape[0]
        sources = route_ref.shape[0]
        bucket = rows // sources
        column = owner_column(owner_ref[0], route_ref[...])
        source = lax.broadcasted_iota(jnp.int32, (sources, rows), 0)
        row = lax.broadcasted_iota(jnp.int32, (sources, rows), 1)
        before = jnp.sum(
            jnp.where(source * bucket + bucket <= row, column, 0), axis=0, keepdims=True
        )
        own = (source * bucket <= row) & (row < source * bucket + bucket)
        count = jnp.sum(jnp.where(own, column, 0), axis=0, keepdims=True)
        place = lax.rem(lax.broadcasted_iota(jnp.int32, (1, rows), 1), bucket)
        target = jnp.where(place < count, before + place, -1)
        slot = lax.broadcasted_iota(jnp.int32, (rows, rows), 0)
        select = jnp.where(slot == target, 1.0, 0.0).astype(BF16)
        pick_ref[...] = jnp.dot(
            select, arrived_ref[...], preferred_element_type=F32
        ).astype(BF16)

    out_ref[0, 0] = jnp.dot(
        pick_ref[...], w_ref[...], preferred_element_type=F32
    ).astype(BF16)


def merge_down_rows(owner, route_count, arrived, merge_down, tp, grp):
    rows, units = arrived.shape
    width = merge_down.shape[1] // (tp * grp)
    return pl.pallas_call(
        down_kernel,
        grid=(tp * grp,),
        in_specs=[
            SMEM,
            VMEM,
            VMEM,
            pl.BlockSpec((units, width), lambda k: (0, k)),
        ],
        out_specs=pl.BlockSpec((1, 1, rows, width), lambda k: (k % grp, k // grp, 0, 0)),
        out_shape=jax.ShapeDtypeStruct((grp, tp, rows, width), BF16),
        scratch_shapes=[pltpu.VMEM((rows, units), BF16)],
        compiler_params=params("arbitrary"),
        name="merge_down",
    )(owner, route_count, arrived, merge_down)


def pair_kernel(parts_ref, out_ref):
    out_ref[...] = (parts_ref[0].astype(F32) + parts_ref[1].astype(F32)).astype(BF16)


def pair_sum(parts):
    return pl.pallas_call(
        pair_kernel,
        in_specs=[VMEM],
        out_specs=VMEM,
        out_shape=jax.ShapeDtypeStruct(parts.shape[1:], BF16),
        compiler_params=params(),
        name="pair_sum",
    )(parts)


def place_kernel(owner_ref, route_ref, parts_ref, text_ref, out_ref):
    total = parts_ref[0].astype(F32)
    for k in range(1, parts_ref.shape[0]):
        total += parts_ref[k].astype(F32)
    visual = jnp.sum(owner_column(owner_ref[0], route_ref[...]), axis=0, keepdims=True)
    slot = lax.broadcasted_iota(jnp.int32, total.shape, 0)
    placed = jnp.where(slot < visual, total, text_ref[...].astype(F32)).astype(BF16)
    for k in range(out_ref.shape[0]):
        out_ref[k] = placed


def place_rows(owner, route_count, parts, text_states):
    return pl.pallas_call(
        place_kernel,
        in_specs=[SMEM, VMEM, VMEM, VMEM],
        out_specs=VMEM,
        out_shape=jax.ShapeDtypeStruct(parts.shape, BF16),
        compiler_params=params(),
        name="place",
    )(owner, route_count, parts, text_states)


def project_kernel(parts_ref, gain_ref, wq_ref, wkv_ref, q_ref, kv_ref):
    grp, tp, rows, width = parts_ref.shape
    squares = jnp.zeros((rows, width), F32)
    for g in range(grp):
        for t in range(tp):
            x = parts_ref[g, t].astype(F32)
            squares += x * x
    mean = jnp.sum(squares, axis=-1, keepdims=True) / (grp * tp * width)
    scale = lax.rsqrt(mean + EPSILON)
    q = jnp.zeros((rows, wq_ref.shape[1]), F32)
    kv = jnp.zeros((rows, wkv_ref.shape[1]), F32)
    for t in range(tp):
        for g in range(grp):
            lo = (t * grp + g) * width
            gain = gain_ref[:, lo : lo + width]
            normal = (parts_ref[g, t].astype(F32) * scale * gain).astype(BF16)
            q += jnp.dot(normal, wq_ref[lo : lo + width, :], preferred_element_type=F32)
            kv += jnp.dot(normal, wkv_ref[lo : lo + width, :], preferred_element_type=F32)
    q = q.astype(BF16)
    kv = kv.astype(BF16)
    for k in range(q_ref.shape[0]):
        q_ref[k] = q
    for k in range(kv_ref.shape[0]):
        kv_ref[k] = kv


def project(parts, norm_gain, query_weight, kv_weight, q_copies, kv_copies):
    rows = parts.shape[2]
    return pl.pallas_call(
        project_kernel,
        in_specs=[VMEM] * 4,
        out_specs=[VMEM] * 2,
        out_shape=[
            jax.ShapeDtypeStruct((q_copies, rows, query_weight.shape[1]), BF16),
            jax.ShapeDtypeStruct((kv_copies, rows, kv_weight.shape[1]), BF16),
        ],
        compiler_params=params(),
        name="project",
    )(parts, norm_gain.reshape(1, -1), query_weight, kv_weight)


def attend_kernel(home_ref, visual_ref, q_ref, kv_ref, seg_ref, out_ref):
    _, rows, q_width = q_ref.shape
    q_blocks = pl.num_programs(0)
    kv_blocks = kv_ref.shape[0]
    heads = q_width // HD
    row_home = home_ref[0]
    column_home = home_ref[1]
    block = pl.program_id(0)
    q_block = row_home * q_blocks + block
    lanes = lax.broadcasted_iota(jnp.int32, (rows, rows), 1)
    q_seg = jnp.broadcast_to(seg_ref[pl.ds(q_block, 1), :], (rows, rows)).T
    q_pos = q_block * rows + lax.broadcasted_iota(jnp.int32, (rows, rows), 0)
    q = jnp.concatenate([q_ref[0, :, h * HD : (h + 1) * HD] for h in range(heads)], axis=0)
    scores = []
    top = None
    for k in range(kv_blocks):
        k_block = k * q_blocks + column_home
        seen_from = jnp.where(lanes < visual_ref[k_block], -1, k_block * rows + lanes)
        k_seg = seg_ref[pl.ds(k_block, 1), :]
        allowed = (q_seg == k_seg) & (seen_from <= q_pos)
        s = lax.dot_general(
            q, kv_ref[k, :, :HD], (((1,), (1,)), ((), ())), preferred_element_type=F32
        ) * (HD**-0.5 * LOG2E)
        s = jnp.concatenate(
            [jnp.where(allowed, s[h * rows : (h + 1) * rows], NEGATIVE) for h in range(heads)],
            axis=0,
        )
        scores.append(s)
        top = s if top is None else jnp.maximum(top, s)
    top = jnp.max(top, axis=1, keepdims=True)
    floor = jnp.maximum(top, 0.5 * NEGATIVE)
    total = jnp.zeros((heads * rows, rows), F32)
    mixed = jnp.zeros((heads * rows, HD), F32)
    for k in range(kv_blocks):
        weights = jnp.exp2(scores[k] - floor)
        total += weights
        mixed += jnp.dot(
            weights.astype(BF16), kv_ref[k, :, HD:], preferred_element_type=F32
        )
    total = jnp.sum(total, axis=1, keepdims=True)
    empty = total == 0.0
    mixed = mixed / jnp.where(empty, 1.0, total)
    mass = jnp.where(empty, NEGATIVE, floor + jnp.log2(jnp.where(empty, 1.0, total)))
    for h in range(heads):
        cols = slice(h * HD, (h + 1) * HD)
        part = slice(h * rows, (h + 1) * rows)
        out_ref[0, :rows, cols] = mixed[part].astype(BF16)
        flat = jnp.broadcast_to(mass[part], (rows, rows)).T[:16]
        high = flat.astype(BF16).astype(F32)
        low = flat - high
        second = lax.broadcasted_iota(jnp.int32, flat.shape, 0) >= 8
        out_ref[0, rows:, cols] = jnp.where(second, low, high).astype(BF16)


def attend(home, visual_count, q_parts, kv_parts, segment_rows):
    q_blocks, rows, width = q_parts.shape
    return pl.pallas_call(
        attend_kernel,
        grid=(q_blocks,),
        in_specs=[
            SMEM,
            SMEM,
            pl.BlockSpec((1, rows, width), lambda k: (k, 0, 0)),
            VMEM,
            VMEM,
        ],
        out_specs=pl.BlockSpec((1, rows + 16, width), lambda k: (k, 0, 0)),
        out_shape=jax.ShapeDtypeStruct((q_blocks, rows + 16, width), BF16),
        compiler_params=params("arbitrary"),
        name="attend",
    )(home, visual_count, q_parts, kv_parts, segment_rows)


def combine_kernel(parts_ref, out_ref):
    count = parts_ref.shape[0]
    rows, width = out_ref.shape
    for h in range(width // HD):
        cols = slice(h * HD, (h + 1) * HD)
        masses = []
        for k in range(count):
            stats = parts_ref[k, rows:, cols].astype(F32)
            flat = stats[0:1] + stats[8:9]
            masses.append(jnp.broadcast_to(flat, (rows, HD)).T)
        top = functools.reduce(jnp.maximum, masses)
        total = jnp.zeros((rows, HD), F32)
        mixed = jnp.zeros((rows, HD), F32)
        for k in range(count):
            weight = jnp.exp2(masses[k] - top)
            total += weight
            mixed += weight * parts_ref[k, :rows, cols].astype(F32)
        out_ref[:, cols] = (mixed / total).astype(BF16)


def combine(parts):
    return pl.pallas_call(
        combine_kernel,
        in_specs=[VMEM],
        out_specs=VMEM,
        out_shape=jax.ShapeDtypeStruct((parts.shape[1] - 16, parts.shape[2]), BF16),
        compiler_params=params(),
        name="combine",
    )(parts)


def shards(
    patches,
    route_count,
    text_states,
    segment_ids,
    vision_gain,
    merge_up,
    merge_down,
    norm_gain,
    query_weight,
    kv_weight,
):
    tp, grp = lax.axis_size("tp"), lax.axis_size("grp")
    n_y, n_x = lax.axis_size("ctx_0"), lax.axis_size("ctx_1")
    y, x = lax.axis_index("ctx_0"), lax.axis_index("ctx_1")
    rows = patches.shape[0]
    home = jnp.stack([y, x]).astype(jnp.int32)
    owner = (y * n_x + x).astype(jnp.int32).reshape(1)
    visual_count = jnp.sum(route_count, axis=0)
    segment_rows = segment_ids.reshape(-1, rows)

    hidden = merge_up_rows(patches, vision_gain, merge_up)
    units = hidden.shape[1]
    hidden = hidden.reshape(n_y, n_x, rows // (n_y * n_x), units)
    hidden = exchange(hidden, "ctx_0", 0)
    hidden = exchange(hidden, "ctx_1", 1)
    partial_sums = merge_down_rows(
        owner, route_count, hidden.reshape(rows, units), merge_down, tp, grp
    )
    partial_sums = pair_sum(exchange(partial_sums, "grp"))
    partial_sums = exchange(partial_sums, "tp")
    placed = place_rows(owner, route_count, partial_sums, text_states)
    packed = exchange(placed, "tp")
    packed = exchange(jnp.broadcast_to(packed[None], (grp, *packed.shape)), "grp")
    packed = packed.reshape(grp, tp, rows, -1)
    q, kv = project(packed, norm_gain, query_weight, kv_weight, n_x, n_y)
    kv = exchange(kv, "ctx_0")
    q = exchange(q, "ctx_1")
    parts = attend(home, visual_count, q, kv, segment_rows)
    return combine(exchange(parts, "ctx_1"))


def solution(mesh):
    finer = Mesh(
        mesh.devices.reshape(8, 8, mesh.shape["tp"], mesh.shape["grp"]),
        ("ctx_0", "ctx_1", "tp", "grp"),
    )
    ctx = ("ctx_0", "ctx_1")
    return jax.shard_map(
        shards,
        mesh=finer,
        in_specs=(
            P(ctx, None),
            P(),
            P(ctx, ("tp", "grp")),
            P(),
            P(),
            P(None, ("tp", "grp")),
            P(("tp", "grp"), None),
            P(),
            P(None, ("tp", "grp")),
            P(None, "tp"),
        ),
        out_specs=P(ctx, ("tp", "grp")),
        check_vma=False,
    )
```

time: 268 us -> 183 us (0.68); the launches traced: 264 us -> 182 us
  local copies, waits for them, and re-layouts: 74.8 us -> 7.29 us
  blocking collectives: 56.1 us -> 123 us
  waiting for transfers between devices: 57.9 us -> 25 us
  starting transfers between devices: 31.5 us -> 9.97 us
  Pallas kernels: 0 us -> 16.6 us
  other arithmetic: 16.5 us -> 0.1 us
  between operations: 13.7 us -> 0.12 us
  matrix products: 13.5 us -> 0 us
    all_to_all x1 -> x7, blocking collectives: 34.5 us -> 123 us  [exchange(): lax.all_to_all(parts, axis, split_axis=dim, concat_axis=dim, tiled=True)]
    gather x3 -> x0, local copies, waits for them, and re-layouts: 47.5 us -> none  [the longest x1 45.5 us: attend(): key_seg = segment_ids[key_pos]]
    all_to_all x2, waiting for transfers between devices: 57.8 us -> 25 us  [exchange(): lax.all_to_all(parts, axis, split_axis=dim, concat_axis=dim, tiled=True)]
    all_gather x1 -> x0, blocking collectives: 21.6 us -> none  [gather_in_order(): parts = lax.all_gather(parts, axes[k], axis=0, tiled=True)]
    all_to_all x2, starting transfers between devices: 31.5 us -> 9.97 us  [exchange(): lax.all_to_all(parts, axis, split_axis=dim, concat_axis=dim, tiled=True)]
    pallas_call x0 -> x7, Pallas kernels: none -> 16.6 us  [the longest x1 8.55 us: attend(): pl.pallas_call(attend_kernel, grid=(q_blocks,), in_specs=[SMEM, SMEM, pl....]
    dot_general x5 -> x0, matrix products: 13.5 us -> none  [the longest x1 5.63 us: shards(): jnp.dot(hidden, merge_down, preferred_element_type=jnp.float32)]
    another operation x1 -> x0, local copies, waits for them, and re-layouts: 7.4 us -> none  [attend(): kv_split = shard_piece.reshape(piece_rows, kv_heads, 2, HD)]
  transfers between devices with their start and end apart: 3 -> 2, of which waited for: 2 -> 2; matrix products, arithmetic and copies ran while one was open for 21% -> 0% of each run, Pallas kernels for 0% -> 0%
where the time goes in v1:
time: 183 us; the launch traced here: 182 us
  blocking collectives  123 us (67%)
  waiting for transfers between devices  25 us (14%)
  Pallas kernels  16.6 us (9%)
  starting transfers between devices  9.97 us (5%)
  local copies, waits for them, and re-layouts  7.29 us (4%)
    all_to_all x7, blocking collectives, exchange(): lax.all_to_all(parts, axis, split_axis=dim, concat_axis=dim, tiled=True)  123 us
    all_to_all x2, waiting for transfers between devices, exchange(): lax.all_to_all(parts, axis, split_axis=dim, concat_axis=dim, tiled=True)  25 us
    all_to_all x2, starting transfers between devices, exchange(): lax.all_to_all(parts, axis, split_axis=dim, concat_axis=dim, tiled=True)  9.97 us
    pallas_call x1, Pallas kernels, attend(): pl.pallas_call(attend_kernel, grid=(q_blocks,), in_specs=[SMEM, SMEM, pl....  8.55 us
    unnamed x17, local copies, waits for them, and re-layouts  5.66 us
  transfers between devices with their start and end apart: 2, of which 2 were waited for; matrix products, arithmetic and copies ran while one was open for 0% of the time, Pallas kernels for 0%

profile of v1, /device:TPU:1, one launch (start us, length us, event | category | flops | bytes accessed | tf_op | source)
XLA Modules:
  0.0 181.8 jit_solution(18251529507372642730)
XLA Ops:
  0.0 0.7 reshape.20.gain_ref
  0.7 3.0 %copy.13.w_ref = bf16[5120,160]{1,0:T(8,128)(2,1)S(1)} copy(bf16[5120,160]{0,1:T(8,128)(2,1)} %param.15) | data formatting | bytes 3276800 | tf_op args[5]
  3.7 0.0 copy-start.3
  3.7 1.3 copy-done.3
  5.0 1.7 merge_up.1
  6.8 15.1 %all_to_all.45 = bf16[8,8,2,160]{3,2,1,0:T(2,128)(2,1)S(1)} all-to-all(bf16[8,8,2,160]{3,2,1,0:T(2,128)(2,1)S(1)} %reshape.21), channel_id=1, replica_groups=mesh['ctx_0'=8,'ctx_1'=8,'tp'=8,'grp'=2] {'ctx_0'}, dimensions={0} | all-to-all | bytes 81920 | tf_op jit(solution)/shard_map/all_to_all | solution.py:28
  21.9 0.7 copy.14
  22.6 6.5 %all-to-all-start.1 = ((bf16[8,8,2,160]{3,2,0,1:T(2,128)(2,1)}), bf16[8,8,2,160]{3,2,0,1:T(2,128)(2,1)S(1)}, u32[]{:S(2)}, u32[]{:S(2)}) async-start(bf16[8,8,2,160]{3,2,0,1:T(2,128)(2,1)} %copy.14), calls=%async_computation.1 | async-start | bytes 131072 | tf_op jit(solution)/shard_map/all_to_all | solution.py:28
  29.1 7.2 %all-to-all-done.1 = bf16[8,8,2,160]{3,2,0,1:T(2,128)(2,1)S(1)} async-done(((bf16[8,8,2,160]{3,2,0,1:T(2,128)(2,1)}), bf16[8,8,2,160]{3,2,0,1:T(2,128)(2,1)S(1)}, u32[]{:S(2)}, u32[]{:S(2)}) %all-to-all-start.1) | async-done | bytes 40992 | tf_op jit(solution)/shard_map/all_to_all | solution.py:28
  36.3 0.1 reshape.22.arrived_ref
  36.4 0.0 copy-done.4
  36.4 0.0 copy-start.2
  36.4 1.3 copy-done.2
  37.7 3.1 %merge_down.1 = bf16[2,8,128,256]{3,2,1,0:T(8,128)(2,1)S(1)} custom-call(s32[1]{0:T(128)} %bitcast.2.owner_ref, s32[64,64]{1,0:T(8,128)S(1)} %copy-done.4, bf16[128,160]{1,0:T(8,128)(2,1)S(1)} %reshape.22.arrived_ref, bf16[160,4096]{1,0:T(8,128)(2,1)S(1)} %copy-done.2), custom_call_target="tpu_custom_call" | custom-call | tf_op jit(solution)/shard_map/merge_down/pallas_call | solution.py:109
  40.9 0.0 copy-start.5
  40.9 12.0 %all_to_all.46.parts_ref = bf16[2,8,128,256]{3,2,1,0:T(8,128)(2,1)S(1)} all-to-all(bf16[2,8,128,256]{3,2,1,0:T(8,128)(2,1)S(1)} %merge_down.1), channel_id=1, replica_groups=mesh['ctx_0'=8,'ctx_1'=8,'tp'=8,'grp'=2] {'grp'}, dimensions={0} | all-to-all | bytes 2097152 | tf_op jit(solution)/shard_map/all_to_all | solution.py:28
  52.9 0.1 pair_sum.1
  53.0 28.8 %all_to_all.47.parts_ref = bf16[8,128,256]{2,1,0:T(8,128)(2,1)S(1)} all-to-all(bf16[8,128,256]{2,1,0:T(8,128)(2,1)S(1)} %pair_sum.1), channel_id=1, replica_groups=mesh['ctx_0'=8,'ctx_1'=8,'tp'=8,'grp'=2] {'tp'}, dimensions={0} | all-to-all | bytes 1048576 | tf_op jit(solution)/shard_map/all_to_all | solution.py:28
  81.8 0.0 copy-done.5
  81.8 0.2 place.1
  82.0 0.0 copy-start.1
  82.0 17.7 %all_to_all.48 = bf16[8,128,256]{2,1,0:T(8,128)(2,1)S(1)} all-to-all(bf16[8,128,256]{2,1,0:T(8,128)(2,1)S(1)} %place.1), channel_id=1, replica_groups=mesh['ctx_0'=8,'ctx_1'=8,'tp'=8,'grp'=2] {'tp'}, dimensions={0} | all-to-all | bytes 1048576 | tf_op jit(solution)/shard_map/all_to_all | solution.py:28
  99.6 0.1 broadcast_in_dim.2
  99.7 7.7 %all_to_all.49.parts_ref = bf16[2,8,128,256]{3,2,1,0:T(8,128)(2,1)S(1)} all-to-all(bf16[2,8,128,256]{3,2,1,0:T(8,128)(2,1)S(1)} %broadcast_in_dim.2), channel_id=1, replica_groups=mesh['ctx_0'=8,'ctx_1'=8,'tp'=8,'grp'=2] {'grp'}, dimensions={0} | all-to-all | bytes 2097152 | tf_op jit(solution)/shard_map/all_to_all | solution.py:28
  107.4 1.8 project.1
  109.2 20.5 %all_to_all.50.q_ref = bf16[8,128,256]{2,1,0:T(8,128)(2,1)S(1)} all-to-all(bf16[8,128,256]{2,1,0:T(8,128)(2,1)S(1)} %get-tuple-element.7), channel_id=1, replica_groups=mesh['ctx_0'=8,'ctx_1'=8,'tp'=8,'grp'=2] {'ctx_1'}, dimensions={0} | all-to-all | bytes 1048576 | tf_op jit(solution)/shard_map/all_to_all | solution.py:28
  129.7 3.5 %all-to-all-start.7 = ((bf16[8,128,256]{2,1,0:T(8,128)(2,1)}), bf16[8,128,256]{2,1,0:T(8,128)(2,1)S(1)}, u32[]{:S(2)}, u32[]{:S(2)}) async-start(bf16[8,128,256]{2,1,0:T(8,128)(2,1)} %get-tuple-element.8), calls=%async_computation.7 | async-start | bytes 1048576 | tf_op jit(solution)/shard_map/all_to_all | solution.py:28
  133.2 0.1 pad_add_fusion.home_ref
  133.3 17.8 %all-to-all-done.7.kv_ref = bf16[8,128,256]{2,1,0:T(8,128)(2,1)S(1)} async-done(((bf16[8,128,256]{2,1,0:T(8,128)(2,1)}), bf16[8,128,256]{2,1,0:T(8,128)(2,1)S(1)}, u32[]{:S(2)}, u32[]{:S(2)}) %all-to-all-start.7) | async-done | bytes 524320 | tf_op jit(solution)/shard_map/all_to_all | solution.py:28
  151.1 8.5 %attend.1 = bf16[8,144,256]{2,1,0:T(8,128)(2,1)S(1)} custom-call(s32[2]{0:T(128)S(1)} %pad_add_fusion.home_ref, s32[64]{0:T(128)S(1)} %reduce_sum.9.visual_ref, bf16[8,128,256]{2,1,0:T(8,128)(2,1)S(1)} %all_to_all.50.q_ref, bf16[8,128,256]{2,1,0:T(8,128)(2,1)S(1)} %all-to-all-done.7.kv_ref, s32[64,128]{1,0:T(8,128)S(1)} %bitcast.5), custom_call_target="tpu_custom_call" | custom-call | tf_op jit(solution)/shard_map/attend/pallas_call | solution.py:260
  159.6 21.1 %all_to_all.51.parts_ref = bf16[8,144,256]{2,1,0:T(8,128)(2,1)S(1)} all-to-all(bf16[8,144,256]{2,1,0:T(8,128)(2,1)S(1)} %attend.1), channel_id=1, replica_groups=mesh['ctx_0'=8,'ctx_1'=8,'tp'=8,'grp'=2] {'ctx_1'}, dimensions={0} | all-to-all | bytes 1179648 | tf_op jit(solution)/shard_map/all_to_all | solution.py:28
  180.7 1.1 combine.1
  (11 shorter events, 0.1 us)
Async XLA Ops:
  3.7 1.3 copy-start.3
  5.0 31.4 %copy-start.4 = (s32[64,64]{1,0:T(8,128)S(1)}, s32[64,64]{1,0:T(8,128)}, u32[]{:S(2)}) copy-start(s32[64,64]{1,0:T(8,128)} %route_ref.3) | copy-start | bytes 49156
  22.6 13.7 %all-to-all-start.1 = ((bf16[8,8,2,160]{3,2,0,1:T(2,128)(2,1)}), bf16[8,8,2,160]{3,2,0,1:T(2,128)(2,1)S(1)}, u32[]{:S(2)}, u32[]{:S(2)}) async-start(bf16[8,8,2,160]{3,2,0,1:T(2,128)(2,1)} %copy.14), calls=%async_computation.1 | async-start | bytes 131072 | tf_op jit(solution)/shard_map/all_to_all | solution.py:28
  36.4 1.3 copy-start.2
  40.9 40.9 %copy-start.5 = (bf16[128,256]{1,0:T(8,128)(2,1)S(1)}, bf16[128,256]{1,0:T(8,128)(2,1)}, u32[]{:S(2)}) copy-start(bf16[128,256]{1,0:T(8,128)(2,1)} %text_ref.1) | copy-start | bytes 196612
  82.0 25.4 %copy-start.1 = (bf16[4096,256]{1,0:T(8,128)(2,1)S(1)}, bf16[4096,256]{1,0:T(8,128)(2,1)}, u32[]{:S(2)}) copy-start(bf16[4096,256]{1,0:T(8,128)(2,1)} %wkv_ref.1) | copy-start | bytes 6291460
  99.6 7.8 %copy-start = (bf16[4096,256]{1,0:T(8,128)(2,1)S(1)}, bf16[4096,256]{1,0:T(8,128)(2,1)}, u32[]{:S(2)}) copy-start(bf16[4096,256]{1,0:T(8,128)(2,1)} %wq_ref.1) | copy-start | bytes 6291460
  99.6 7.8 %copy-start.7 = (f32[4096]{0:T(1024)S(1)}, f32[4096]{0:T(1024)}, u32[]{:S(2)}) copy-start(f32[4096]{0:T(1024)} %param.17) | copy-start | bytes 49156
  109.2 41.8 %copy-start.6 = (s32[8192]{0:T(1024)S(1)}, s32[8192]{0:T(1024)}, u32[]{:S(2)}) copy-start(s32[8192]{0:T(1024)} %param.13) | copy-start | bytes 98308
  129.7 21.4 %all-to-all-start.7 = ((bf16[8,128,256]{2,1,0:T(8,128)(2,1)}), bf16[8,128,256]{2,1,0:T(8,128)(2,1)S(1)}, u32[]{:S(2)}, u32[]{:S(2)}) async-start(bf16[8,128,256]{2,1,0:T(8,128)(2,1)} %get-tuple-element.8), calls=%async_computation.7 | async-start | bytes 1048576 | tf_op jit(solution)/shard_map/all_to_all | solution.py:28
